TPU v7x, 32 devices: a whole 2x2x4 slice. The times are simulated.
32 devices in a mesh: rows: 8 (over z, y), rep: 4 (over x, core).
Axes of the slice: x: 2, y: 2, z: 4, core: 2. Of those that a mesh axis runs over, the one named last changes fastest.
Arguments:
- tables: bfloat16 [16384, 128], P('rows'), may hold values from -0.5 to 0.5
- indices: int32 [512, 8, 8], P(('rows', 'rep')), may hold values from 0 to 2047
- bag_lengths: int32 [512, 8], P(('rows', 'rep')), may hold values from 1 to 8
- dense: bfloat16 [512, 13], P(('rows', 'rep')), may hold values from -6 to 6
- bottom_first: bfloat16 [13, 512], replicated, may hold values from -1.75 to 1.75
- bottom_second: bfloat16 [512, 256], replicated, may hold values from -0.375 to 0.375
- bottom_third: bfloat16 [256, 128], replicated, may hold values from -0.5 to 0.5
- top_first: bfloat16 [164, 1024], P(None, 'rep'), may hold values from -0.5 to 0.5
- top_second: bfloat16 [1024, 1024], P(None, 'rep'), may hold values from -0.25 to 0.25
- top_third: bfloat16 [1024, 512], P(None, 'rep'), may hold values from -0.25 to 0.25
- top_fourth: bfloat16 [512, 256], P(None, 'rep'), may hold values from -0.375 to 0.375
- top_last: bfloat16 [256], replicated, may hold values from -0.5 to 0.5
Outputs:
- logit: float32 [512], P(('rows', 'rep'))
Inputs may be any that keep to these rules, and one draw needn't show every extreme that they name: `indices`: each entry is a row number within its own table; entries at positions of a bag at or past its length are ignored.
All inputs are finite; a program needn't handle non-finite values.
Results may differ from a plain program's by a relative error of at most 0.0076.
Values may be sent and summed in bfloat16 or wider, within the bound.
A program may use at most 64 MiB of HBM per device.

v0:
```python
import jax
import jax.numpy as jnp
import numpy as np
from jax import lax
from jax.sharding import PartitionSpec as P

TAB = 8
HOT = 8


def interact(bottom_out, pooled):
    features = jnp.concatenate([bottom_out[None], pooled], axis=0)
    gram_matrix = jnp.einsum("ibe,jbe->bij", features, features, precision=lax.Precision.HIGHEST)
    left_ids, right_ids = np.triu_indices(TAB + 1, 1)
    pair_dots = gram_matrix[:, left_ids, right_ids]
    return jnp.concatenate([bottom_out, pair_dots], axis=1).astype(jnp.bfloat16)


def bottom_net(dense, bottom_first, bottom_second, bottom_third):
    lower_act = jax.nn.relu(
        jnp.dot(dense, bottom_first, preferred_element_type=jnp.float32)
    ).astype(jnp.bfloat16)
    middle = jax.nn.relu(
        jnp.dot(lower_act, bottom_second, preferred_element_type=jnp.float32)
    ).astype(jnp.bfloat16)
    return jax.nn.relu(jnp.dot(middle, bottom_third, preferred_element_type=jnp.float32))


def body(
    tables,
    indices,
    bag_lengths,
    dense,
    bottom_first,
    bottom_second,
    bottom_third,
    top_first,
    top_second,
    top_third,
    top_fourth,
    top_last,
):
    batch_rows = indices.shape[0]
    row_count = tables.shape[0]
    emb_width = tables.shape[1]
    device_count = lax.axis_size("rows")
    per_table = device_count // TAB
    position = lax.axis_index("rows")
    row_offset = position % per_table * row_count
    slot_ids = jnp.arange(HOT, dtype=jnp.int32)
    masked = jnp.where(slot_ids[None, None, :] < bag_lengths[:, :, None], indices, -1)
    outgoing = jnp.repeat(jnp.transpose(masked, (1, 0, 2)), per_table, axis=0)
    incoming = lax.all_to_all(outgoing, "rows", split_axis=0, concat_axis=0, tiled=True)
    wanted = incoming.reshape(device_count * batch_rows, HOT)
    local_ids = wanted - row_offset
    block_rows = min(512, row_count)
    block_count = row_count // block_rows

    def add_block(block_num, partial_value):
        first_row = block_num * block_rows
        cell_ids = first_row + jnp.arange(block_rows, dtype=jnp.int32)
        counts = jnp.zeros((local_ids.shape[0], block_rows), jnp.float32)
        for slot_num in range(HOT):
            counts = counts + (local_ids[:, slot_num : slot_num + 1] == cell_ids[None, :]).astype(
                jnp.float32
            )
        block_table = lax.dynamic_slice_in_dim(tables, first_row, block_rows, 0)
        return partial_value + jnp.dot(
            counts.astype(jnp.bfloat16), block_table, preferred_element_type=jnp.float32
        )

    partial_value = lax.fori_loop(
        0, block_count, add_block, jnp.zeros((local_ids.shape[0], emb_width), jnp.float32)
    )
    bag_parts = lax.all_to_all(
        partial_value.reshape(device_count, batch_rows, emb_width),
        "rows",
        split_axis=0,
        concat_axis=0,
        tiled=True,
    )
    pooled = jnp.sum(bag_parts.reshape(TAB, per_table, batch_rows, emb_width), axis=1)
    bottom_out = bottom_net(dense, bottom_first, bottom_second, bottom_third)
    activation = interact(bottom_out, pooled)
    whole = (
        lax.all_gather(top_first, "rep", axis=1, tiled=True),
        lax.all_gather(top_second, "rep", axis=1, tiled=True),
        lax.all_gather(top_third, "rep", axis=1, tiled=True),
        lax.all_gather(top_fourth, "rep", axis=1, tiled=True),
    )
    for weight_mat in whole:
        activation = jax.nn.relu(
            jnp.dot(activation, weight_mat, preferred_element_type=jnp.float32)
        ).astype(jnp.bfloat16)
    return jnp.dot(activation, top_last, preferred_element_type=jnp.float32)


def solution(mesh):
    placed = (
        P("rows", None),
        P(("rows", "rep"), None, None),
        P(("rows", "rep"), None),
        P(("rows", "rep"), None),
        P(),
        P(),
        P(),
        P(None, "rep"),
        P(None, "rep"),
        P(None, "rep"),
        P(None, "rep"),
        P(),
    )
    return jax.shard_map(
        body, mesh=mesh, in_specs=placed, out_specs=P(("rows", "rep")), check_vma=False
    )
```

profile of v0, /device:TPU:0, one launch (start us, length us, event | category | flops | bytes accessed | tf_op | source)
XLA Modules:
  0.0 64.0 jit_solution(13387077456647653964)
XLA Ops:
  6.5 0.0 copy-start
  6.5 0.0 all-gather.3.cloned.1.call-start
  6.5 0.7 %all-gather.3.cloned.1.call-update = ((bf16[1024,256]{1,0:T(8,128)(2,1)}), bf16[1024,1024]{1,0:T(8,128)(2,1)}) async-update(((), (), s32[]{:S(2)}) %all-gather.3.cloned.1.call-start, bf16[1024,256]{1,0:T(8,128)(2,1)} %param.26) | async-update | bytes 3145752
  7.3 0.8 %fusion.36 = s32[8,8,16]{2,1,0:T(8,128)S(1)} fusion(s32[16,8,8]{0,2,1:T(8,128)} %param.19, s32[16,8]{0,1:T(8,128)} %param.20), kind=kLoop, calls=%fused_computation.55 | loop fusion | flops 2048 | bytes 8704
  8.0 0.7 %reshape.24 = s32[8,1,128]{2,1,0:T(1,128)} reshape(s32[8,8,16]{2,1,0:T(8,128)S(1)} %fusion.36) | data formatting | bytes 8192
  8.7 7.3 %all-to-all-start = ((s32[8,1,128]{2,1,0:T(1,128)}), s32[8,1,128]{2,1,0:T(1,128)S(1)}, u32[]{:S(2)}, u32[]{:S(2)}) async-start(s32[8,1,128]{2,1,0:T(1,128)} %reshape.24), calls=%async_computation | async-start | bytes 8192 | tf_op jit(solution)/shard_map/all_to_all | solution.py:53
  16.0 0.0 all-gather.5.cloned.1.call-start
  16.1 0.7 %all-gather.5.cloned.1.call-update = ((bf16[1024,128]{1,0:T(8,128)(2,1)}), bf16[1024,512]{1,0:T(8,128)(2,1)}) async-update(((), (), s32[]{:S(2)}) %all-gather.5.cloned.1.call-start, bf16[1024,128]{1,0:T(8,128)(2,1)} %param.27) | async-update | bytes 1572888
  16.8 0.0 copy-done
  16.8 1.0 %fusion.18 = bf16[16,256]{1,0:T(8,128)(2,1)S(1)} fusion(bf16[512,256]{1,0:T(8,128)(2,1)S(1)} %copy-done, bf16[16,13]{1,0:T(8,128)(2,1)} %param.21, bf16[13,512]{1,0:T(8,128)(2,1)} %param.22), kind=kOutput, calls=%fused_computation.35 | convolution fusion | flops 4431872 | bytes 284064 | tf_op jit(solution)/shard_map/dot_general | solution.py:24
  17.7 1.0 %fusion.35 = (bf16[16,128]{1,0:T(8,128)(2,1)S(1)}, f32[16,128]{1,0:T(8,128)S(1)}) fusion(bf16[16,256]{1,0:T(8,128)(2,1)S(1)} %fusion.18, bf16[256,128]{1,0:T(8,128)(2,1)} %param.24), kind=kOutput, calls=%fused_computation.54 | convolution fusion | flops 1052672 | bytes 86016 | tf_op jit(solution)/shard_map/dot_general | solution.py:26
  18.7 7.8 %all_gather.15 = bf16[512,256]{0,1:T(8,128)(2,1)S(1)} all-gather(bf16[512,64]{0,1:T(8,128)(2,1)} %param.28), channel_id=1, replica_groups=mesh['rows'=8,'rep'=4] {'rep'}, dimensions={1}, use_global_device_ids=true | all-gather | bytes 327680 | tf_op jit(solution)/shard_map/all_gather | solution.py:89
  26.5 0.7 %reshape.22 = bf16[256,1]{0,1:T(2,128)(2,1)S(1)} reshape(bf16[256]{0:T(256)(128)(2,1)} %param.29) | data formatting | bytes 1024 | tf_op args[11]
  27.2 0.0 all-to-all-done
  27.2 0.6 broadcast.33
  27.8 0.7 %reduce = s32[8,128]{1,0:T(8,128)S(1)} reduce(s32[8,1,128]{2,1,0:T(1,128)S(1)} %all-to-all-done, s32[]{:T(128)} %broadcast.33), dimensions={1}, to_apply=%all_to_all.6.reduce_sub_computation | reduce | bytes 8196 | tf_op jit(solution)/shard_map/all_to_all | solution.py:53
  28.5 0.1 reshape.25
  28.6 0.1 reshape.14
  28.7 0.0 copy-start.2
  28.7 0.0 copy-start.1
  28.7 7.8 %while.14 = (s32[]{:T(128)}, f32[128,128]{1,0:T(8,128)}, s32[128,8]{0,1:T(8,128)S(1)}, bf16[2048,128]{1,0:T(8,128)(2,1)}, s32[]{:T(128)}, /*index=5*/s32[]{:T(128)}, s32[]{:T(128)}, s32[]{:T(128)}) while((s32[]{:T(128)}, f32[128,128]{1,0:T(8,128)}, s32[128,8]{0,1:T(8,128)S(1)}, bf16[2048,128]{1,0:T(8,128)(2,1)}, s32[]{:T(128)}, ...), condition=%wide.region_1.2_spmd.clone, body=%wide.region_0.1_spmd.clone.sunk | while | flops 18383368 | bytes 278677 | solution.py:72
  28.7 1.9 %convolution_add_fusion.2 = f32[128,128]{1,0:T(8,128)} fusion(bf16[2048,128]{1,0:T(8,128)(2,1)} %get-tuple-element.178, s32[]{:T(128)S(6)} %select_n.30, s32[512]{0:T(512)S(1)} %iota_add_fusion.2, s32[128]{0:T(128)S(1)} %get-tuple-element.151, s32[128]{0:T(128)S(1)} %get-tuple-element.152, s32[128]{0:T(128)S(1)} %get-tuple-element.153, ...), kind=kOutput, calls=%fused_computation.1.clone.1 | convolution fusion | flops 18382848 | bytes 268293 | tf_op jit(solution)/shard_map/while/body/eval_jaxpr/dot_general | solution.py:68
  30.7 1.9 %convolution_add_fusion.2 = f32[128,128]{1,0:T(8,128)} fusion(bf16[2048,128]{1,0:T(8,128)(2,1)} %get-tuple-element.178, s32[]{:T(128)S(6)} %select_n.30, s32[512]{0:T(512)S(1)} %iota_add_fusion.2, s32[128]{0:T(128)S(1)} %get-tuple-element.151, s32[128]{0:T(128)S(1)} %get-tuple-element.152, s32[128]{0:T(128)S(1)} %get-tuple-element.153, ...), kind=kOutput, calls=%fused_computation.1.clone.1 | convolution fusion | flops 18382848 | bytes 268293 | tf_op jit(solution)/shard_map/while/body/eval_jaxpr/dot_general | solution.py:68
  32.6 1.9 %convolution_add_fusion.2 = f32[128,128]{1,0:T(8,128)} fusion(bf16[2048,128]{1,0:T(8,128)(2,1)} %get-tuple-element.178, s32[]{:T(128)S(6)} %select_n.30, s32[512]{0:T(512)S(1)} %iota_add_fusion.2, s32[128]{0:T(128)S(1)} %get-tuple-element.151, s32[128]{0:T(128)S(1)} %get-tuple-element.152, s32[128]{0:T(128)S(1)} %get-tuple-element.153, ...), kind=kOutput, calls=%fused_computation.1.clone.1 | convolution fusion | flops 18382848 | bytes 268293 | tf_op jit(solution)/shard_map/while/body/eval_jaxpr/dot_general | solution.py:68
  34.5 2.0 %convolution_add_fusion.2 = f32[128,128]{1,0:T(8,128)} fusion(bf16[2048,128]{1,0:T(8,128)(2,1)} %get-tuple-element.178, s32[]{:T(128)S(6)} %select_n.30, s32[512]{0:T(512)S(1)} %iota_add_fusion.2, s32[128]{0:T(128)S(1)} %get-tuple-element.151, s32[128]{0:T(128)S(1)} %get-tuple-element.152, s32[128]{0:T(128)S(1)} %get-tuple-element.153, ...), kind=kOutput, calls=%fused_computation.1.clone.1 | convolution fusion | flops 18382848 | bytes 268293 | tf_op jit(solution)/shard_map/while/body/eval_jaxpr/dot_general | solution.py:68
  36.5 6.0 %all-to-all-start.1 = ((f32[8,16,128]{2,1,0:T(8,128)}), f32[8,16,128]{2,1,0:T(8,128)S(1)}, u32[]{:S(2)}, u32[]{:S(2)}) async-start(f32[8,16,128]{2,1,0:T(8,128)} %bitcast.2), calls=%async_computation.1 | async-start | bytes 131072 | tf_op jit(solution)/shard_map/all_to_all | solution.py:75
  42.5 0.0 copy-done.2
  42.5 7.2 %all_gather.12 = bf16[164,1024]{1,0:T(8,128)(2,1)S(1)} all-gather(bf16[164,256]{1,0:T(8,128)(2,1)S(1)} %copy-done.2), channel_id=1, replica_groups=mesh['rows'=8,'rep'=4] {'rep'}, dimensions={1}, use_global_device_ids=true | all-gather | bytes 419840 | tf_op jit(solution)/shard_map/all_gather | solution.py:86
  49.7 0.0 all-to-all-done.1
  49.7 0.3 fusion.19
  50.1 0.1 copy.20
  50.2 0.0 copy-done.1
  50.2 1.0 %gather_fusion = bf16[36,16]{1,0:T(8,128)(2,1)S(1)} fusion(bf16[16,9,9]{0,2,1:T(8,128)(2,1)S(1)} %copy.20, s32[36]{0:T(128)S(1)} %copy-done.1), kind=kCustom, calls=%fused_computation | custom fusion | bytes 2592 | tf_op jit(solution)/shard_map/gather | solution.py:15
  51.3 0.1 copy.18
  51.4 0.0 all-gather.3.cloned.1.call-done
  51.4 2.1 %fusion.11 = bf16[16,1024]{1,0:T(8,128)(2,1)S(1)} fusion(bf16[1024,1024]{1,0:T(8,128)(2,1)} %all-gather.3.cloned.1.call-done, bf16[164,1024]{1,0:T(8,128)(2,1)S(1)} %all_gather.12, bf16[16,36]{1,0:T(8,128)(2,1)S(1)} %bitcast.48, bf16[16,128]{1,0:T(8,128)(2,1)S(1)} %get-tuple-element.116), kind=kOutput, calls=%fused_computation.25 | convolution fusion | flops 39004416 | bytes 2471040 | tf_op jit(solution)/shard_map/dot_general | solution.py:93
  53.5 1.5 %all-gather.5.cloned.1.call-done = bf16[1024,512]{1,0:T(8,128)(2,1)} async-done(((bf16[1024,128]{1,0:T(8,128)(2,1)}), bf16[1024,512]{1,0:T(8,128)(2,1)}) %all-gather.5.cloned.1.call-update) | async-done | bytes 1048592 | tf_op jit(solution)/shard_map/all_gather | solution.py:88
  55.0 1.6 %fusion.17 = bf16[16,256]{1,0:T(8,128)(2,1)S(1)} fusion(bf16[512,256]{0,1:T(8,128)(2,1)S(1)} %all_gather.15, bf16[16,1024]{1,0:T(8,128)(2,1)S(1)} %fusion.11, bf16[1024,512]{1,0:T(8,128)(2,1)} %all-gather.5.cloned.1.call-done), kind=kOutput, calls=%fused_computation.34 | convolution fusion | flops 20996096 | bytes 1351680 | tf_op jit(solution)/shard_map/dot_general | solution.py:93
  56.5 0.7 %convolution_bitcast_fusion = f32[16]{0:T(128)} fusion(bf16[16,256]{1,0:T(8,128)(2,1)S(1)} %fusion.17, bf16[256,1]{0,1:T(2,128)(2,1)S(1)} %reshape.22), kind=kOutput, calls=%fused_computation.37 | convolution fusion | flops 8192 | bytes 8768 | tf_op jit(solution)/shard_map/dot_general | solution.py:95
  (11 shorter events, 0.1 us)
Async XLA Ops:
  6.5 10.2 %copy-start = (bf16[512,256]{1,0:T(8,128)(2,1)S(1)}, bf16[512,256]{1,0:T(8,128)(2,1)}, u32[]{:S(2)}) copy-start(bf16[512,256]{1,0:T(8,128)(2,1)} %param.23) | copy-start | bytes 786436
  6.5 44.8 %all-gather.3.cloned.1.call-start = ((), (), s32[]{:S(2)}) async-start(), calls=%async_computation.2 | async-start | bytes 2621440 | tf_op jit(solution)/shard_map/all_gather | solution.py:87
  8.7 18.5 %all-to-all-start = ((s32[8,1,128]{2,1,0:T(1,128)}), s32[8,1,128]{2,1,0:T(1,128)S(1)}, u32[]{:S(2)}, u32[]{:S(2)}) async-start(s32[8,1,128]{2,1,0:T(1,128)} %reshape.24), calls=%async_computation | async-start | bytes 8192 | tf_op jit(solution)/shard_map/all_to_all | solution.py:53
  16.0 38.9 %all-gather.5.cloned.1.call-start = ((), (), s32[]{:S(2)}) async-start(), calls=%async_computation.3 | async-start | bytes 1310720 | tf_op jit(solution)/shard_map/all_gather | solution.py:88
  28.7 13.9 %copy-start.2 = (bf16[164,256]{1,0:T(8,128)(2,1)S(1)}, bf16[164,256]{1,0:T(8,128)(2,1)}, u32[]{:S(2)}) copy-start(bf16[164,256]{1,0:T(8,128)(2,1)} %param.25) | copy-start | bytes 251908
  28.7 21.6 %copy-start.1 = (s32[36]{0:T(128)S(1)}, s32[36]{0:T(128)}, u32[]{:S(2)}) copy-start(s32[36]{0:T(128)} %constant.99) | copy-start | bytes 436
  36.5 13.2 %all-to-all-start.1 = ((f32[8,16,128]{2,1,0:T(8,128)}), f32[8,16,128]{2,1,0:T(8,128)S(1)}, u32[]{:S(2)}, u32[]{:S(2)}) async-start(f32[8,16,128]{2,1,0:T(8,128)} %bitcast.2), calls=%async_computation.1 | async-start | bytes 131072 | tf_op jit(solution)/shard_map/all_to_all | solution.py:75
Sparse Core Ops, SparseCore 0:
  8.9 26.9 all-gather.2
  37.4 17.5 all-gather.4
where the time goes:
time: 64.6 us; the launch traced here: 64 us
  blocking collectives  15 us (23%)
  matrix products  14.3 us (22%)
  between operations  13.5 us (21%)
  starting transfers between devices  13.4 us (21%)
  local copies, waits for them, and re-layouts  3.4 us (5%)
  waiting for transfers between devices  2.91 us (5%)
  other arithmetic  1.49 us (2%)
    all_gather x1, blocking collectives, body(): lax.all_gather(top_fourth, 'rep', axis=1, tiled=True)  7.79 us
    dot_general x4, matrix products, add_block(): jnp.dot(counts.astype(jnp.bfloat16), block_table, preferred_element_type=...  7.73 us
    all_to_all x1, starting transfers between devices, body(): lax.all_to_all(outgoing, 'rows', split_axis=0, concat_axis=0, tiled=True)  7.31 us
    all_gather x1, blocking collectives, body(): lax.all_gather(top_first, 'rep', axis=1, tiled=True)  7.18 us
    all_to_all x1, starting transfers between devices, body(): lax.all_to_all(partial_value.reshape(device_count, batch_rows, emb_width)...  6.03 us
    dot_general x2, matrix products, body(): jnp.dot(activation, weight_mat, preferred_element_type=jnp.float32)  3.66 us
    all_gather x1, waiting for transfers between devices, body(): lax.all_gather(top_third, 'rep', axis=1, tiled=True)  1.5 us
    unnamed x9, local copies, waits for them, and re-layouts  1.42 us
  transfers between devices with their start and end apart: 4, of which 1 were waited for; matrix products, arithmetic and copies ran while one was open for 27% of the time, Pallas kernels for 0%

commit v1 on v0

v1 whole, which is shorter than its diff:
```python
import functools

import jax
import jax.numpy as jnp
from jax import lax
from jax.experimental import pallas as pl
from jax.experimental.pallas import tpu as pltpu
from jax.sharding import PartitionSpec as P

TAB = 8
HOT = 8
MESH = pl.DeviceIdType.MESH
BF16 = jnp.bfloat16
F32 = jnp.float32


def flip(k, offset):
    bit = 1
    while bit <= offset:
        if offset & bit:
            k = k + bit - 2 * bit * ((k // bit) % 2)
        bit *= 2
    return k


def dot(a, b):
    return jnp.dot(a, b, preferred_element_type=F32)


def dot_t(a, b):
    return lax.dot_general(a, b, (((1,), (1,)), ((), ())), preferred_element_type=F32)


def relu_round(x):
    return jnp.maximum(x, 0.0).astype(BF16)


def kernel(
    D,
    R,
    tables,
    indices_h,
    lengths_h,
    dense_h,
    bottom_first_h,
    bottom_second_h,
    bottom_third_h,
    top_first,
    top_second,
    top_third,
    top_fourth,
    top_last_h,
    out,
    indices,
    bag_lengths,
    dense,
    bottom_first,
    bottom_second,
    bottom_third,
    top_last,
    table_v,
    w1,
    w2,
    w3,
    w4,
    out_idx,
    recv_idx,
    counts,
    part,
    recv_pool,
    recv_top,
    act1,
    act2,
    recv_act2,
    local_sem,
    e1_send,
    e1_recv,
    e2_send,
    e2_recv,
    e3_send,
    e3_recv,
    e4_send,
    e4_recv,
    w_send,
    w_recv,
):
    B = indices.shape[2]
    rows = tables.shape[0]
    per_table = D // TAB
    me = lax.axis_index("rows")
    k = lax.axis_index("rep")

    barrier = pltpu.get_barrier_semaphore()
    for d in range(1, D):
        pl.semaphore_signal(
            barrier, inc=1, device_id=(lax.rem(me + d, D), k), device_id_type=MESH
        )
    for o in range(1, R):
        pl.semaphore_signal(barrier, inc=1, device_id=(me, flip(k, o)), device_id_type=MESH)

    small = [
        pltpu.make_async_copy(indices_h, indices, local_sem.at[5]),
        pltpu.make_async_copy(lengths_h, bag_lengths, local_sem.at[6]),
        pltpu.make_async_copy(dense_h, dense, local_sem.at[7]),
        pltpu.make_async_copy(bottom_first_h, bottom_first, local_sem.at[8]),
        pltpu.make_async_copy(bottom_second_h, bottom_second, local_sem.at[9]),
        pltpu.make_async_copy(bottom_third_h, bottom_third, local_sem.at[10]),
        pltpu.make_async_copy(top_last_h, top_last, local_sem.at[11]),
    ]
    local = [
        pltpu.make_async_copy(tables, table_v, local_sem.at[0]),
        pltpu.make_async_copy(top_first, w1.at[k], local_sem.at[1]),
        pltpu.make_async_copy(top_second, w2, local_sem.at[2]),
        pltpu.make_async_copy(top_third, w3.at[k], local_sem.at[3]),
        pltpu.make_async_copy(top_fourth, w4.at[k], local_sem.at[4]),
    ]
    for copy in small + local:
        copy.start()

    small[0].wait()
    small[1].wait()
    lens = bag_lengths[...]
    out_idx[...] = jnp.concatenate(
        [jnp.where(lens > s, indices[:, s, :], -1) for s in range(HOT)], axis=1
    ).reshape(TAB, 1, B * HOT)

    pl.semaphore_wait(barrier, D - 1 + R - 1)

    sends = []

    def send(src, dst, ssem, rsem, device):
        copy = pltpu.make_async_remote_copy(
            src_ref=src,
            dst_ref=dst,
            send_sem=ssem,
            recv_sem=rsem,
            device_id=device,
            device_id_type=MESH,
        )
        copy.start()
        sends.append(copy)
        return copy

    first = []
    for d in range(1, D):
        peer = lax.rem(me + d, D)
        first.append(
            send(
                out_idx.at[peer // per_table],
                recv_idx.at[me],
                e1_send.at[d],
                e1_recv.at[d],
                (peer, k),
            )
        )
    recv_idx[me] = out_idx[me // per_table]

    mine = (top_first, top_third, top_fourth)
    whole = (w1, w3, w4)
    arriving = {}
    stages = []
    held = [0]
    bit = R // 2
    while bit:
        stages.append([(bit, h) for h in held])
        held = held + [h ^ bit for h in held]
        bit //= 2

    def weight_send(array, bit, h):
        block = flip(k, h)
        src = mine[array] if h == 0 else whole[array].at[block]
        arriving[array, h ^ bit] = send(
            src,
            whole[array].at[block],
            w_send.at[array * R + (h ^ bit)],
            w_recv.at[array * R + (h ^ bit)],
            (me, flip(k, bit)),
        )

    for array in range(3):
        for stage in stages:
            for bit, h in stage:
                if h == 0:
                    weight_send(array, bit, h)

    got = set()

    def weight_forward(array):
        for stage in stages:
            for bit, h in stage:
                if h != 0:
                    if (array, h) not in got:
                        arriving[array, h].wait_recv()
                        got.add((array, h))
                    weight_send(array, bit, h)

    def weight_finish(array):
        for o in range(1, R):
            if (array, o) not in got:
                arriving[array, o].wait_recv()
                got.add((array, o))

    for copy in small[2:]:
        copy.wait()
    lower = relu_round(dot(dense[...], bottom_first[...]))
    middle = relu_round(dot(lower, bottom_second[...]))
    bottom_out = jnp.maximum(dot(middle, bottom_third[...]), 0.0)

    local[0].wait()
    for copy in first:
        copy.wait_recv()

    offset = (me % per_table) * rows
    cells = lax.broadcasted_iota(jnp.int32, (8, rows), 1)

    def group(g):
        wanted = recv_idx[pl.ds(g * 8, 8)].reshape(8, B * HOT) - offset
        for pair in range(B // 2):
            halves = []
            for b in (2 * pair, 2 * pair + 1):
                total = jnp.zeros((8, rows), F32)
                for s in range(HOT):
                    j = B * s + b
                    total = total + jnp.where(wanted[:, j : j + 1] == cells, 1.0, 0.0)
                halves.append(total)
            counts[16 * pair : 16 * pair + 16, :] = jnp.concatenate(halves, axis=0).astype(BF16)
        partial = dot(counts[...], table_v[...])
        for b in range(B):
            part[pl.ds(g * 8, 8), b, :] = partial[8 * b : 8 * b + 8, :]

    if D == 8:
        group(0)
    else:
        pl.loop(0, D // 8)(group)

    second = []
    for d in range(1, D):
        peer = lax.rem(me + d, D)
        second.append(
            send(part.at[peer], recv_pool.at[me], e2_send.at[d], e2_recv.at[d], (peer, k))
        )
    recv_pool[me] = part[me]
    weight_forward(0)
    for copy in second:
        copy.wait_recv()

    features = [bottom_out]
    for t in range(TAB):
        pooled = recv_pool[t * per_table]
        for i in range(1, per_table):
            pooled = pooled + recv_pool[t * per_table + i]
        features.append(pooled)
    E = bottom_out.shape[1]
    lane = lax.broadcasted_iota(jnp.int32, (B, E), 1)
    dots = jnp.zeros((B, E), F32)
    p = 0
    for i in range(TAB + 1):
        for j in range(i + 1, TAB + 1):
            value = jnp.sum(features[i] * features[j], axis=1, keepdims=True)
            dots = jnp.where(lane == p, value, dots)
            p += 1
    recv_top[k] = jnp.concatenate([bottom_out, dots], axis=1).astype(BF16)

    third = [
        send(recv_top.at[k], recv_top.at[k], e3_send.at[o], e3_recv.at[o], (me, flip(k, o)))
        for o in range(1, R)
    ]
    weight_finish(0)
    weight_forward(1)
    weight_forward(2)
    for copy in local[1:]:
        copy.wait()
    for copy in third:
        copy.wait_recv()

    top_in = recv_top[...].reshape(R * B, 2 * E)
    n1 = w1.shape[2]
    for n in range(R):
        act1[:, n * n1 : (n + 1) * n1] = relu_round(
            dot(top_in[:, :E], w1[n, :E, :]) + dot(top_in[:, E : E + p], w1[n, E:, :])
        )
    act2[...] = relu_round(dot(act1[...], w2[...])).reshape(act2.shape)

    fourth = [
        send(
            act2.at[flip(k, o)], recv_act2.at[k], e4_send.at[o], e4_recv.at[o], (me, flip(k, o))
        )
        for o in range(1, R)
    ]
    recv_act2[k] = act2[k]
    weight_finish(1)
    weight_finish(2)
    for copy in fourth:
        copy.wait_recv()

    third_in = jnp.concatenate([recv_act2[n] for n in range(R)], axis=1)
    fourth_in = jnp.concatenate([relu_round(dot(third_in, w3[n])) for n in range(R)], axis=1)
    last_in = jnp.concatenate([relu_round(dot_t(fourth_in, w4[n])) for n in range(R)], axis=1)
    out[...] = dot_t(top_last[...].reshape(1, -1), last_in).reshape(B)
    for copy in sends:
        copy.wait_send()


def body(*args):
    (tables, indices, bag_lengths, dense, b1, b2, b3, t1, t2, t3, t4, last) = args
    D = lax.axis_size("rows")
    R = lax.axis_size("rep")
    B = indices.shape[0]
    indices = jnp.transpose(indices, (1, 2, 0))
    bag_lengths = jnp.transpose(bag_lengths)
    t4 = jnp.transpose(t4)
    E = tables.shape[1]
    vmem = pl.BlockSpec(memory_space=pltpu.VMEM)
    hbm = pl.BlockSpec(memory_space=pl.ANY)
    dma = pltpu.SemaphoreType.DMA
    result = pl.pallas_call(
        functools.partial(kernel, D, R),
        out_shape=jax.ShapeDtypeStruct((B,), F32),
        in_specs=[hbm] * 12,
        out_specs=vmem,
        scratch_shapes=[
            pltpu.VMEM(indices.shape, jnp.int32),
            pltpu.VMEM(bag_lengths.shape, jnp.int32),
            pltpu.VMEM(dense.shape, BF16),
            pltpu.VMEM(b1.shape, BF16),
            pltpu.VMEM(b2.shape, BF16),
            pltpu.VMEM(b3.shape, BF16),
            pltpu.VMEM(last.shape, BF16),
            pltpu.VMEM(tables.shape, BF16),
            pltpu.VMEM((R,) + t1.shape, BF16),
            pltpu.VMEM(t2.shape, BF16),
            pltpu.VMEM((R,) + t3.shape, BF16),
            pltpu.VMEM((R,) + t4.shape, BF16),
            pltpu.VMEM((TAB, 1, B * HOT), jnp.int32),
            pltpu.VMEM((D, 1, B * HOT), jnp.int32),
            pltpu.VMEM((8 * B, tables.shape[0]), BF16),
            pltpu.VMEM((D, B, E), F32),
            pltpu.VMEM((D, B, E), F32),
            pltpu.VMEM((R, B, 2 * E), BF16),
            pltpu.VMEM((R * B, R * t1.shape[1]), BF16),
            pltpu.VMEM((R, B, t2.shape[1]), BF16),
            pltpu.VMEM((R, B, t2.shape[1]), BF16),
            dma((12,)),
            dma((D,)),
            dma((D,)),
            dma((D,)),
            dma((D,)),
            dma((R,)),
            dma((R,)),
            dma((R,)),
            dma((R,)),
            dma((3 * R,)),
            dma((3 * R,)),
        ],
        compiler_params=pltpu.CompilerParams(collective_id=0, has_side_effects=True),
    )(tables, indices, bag_lengths, dense, b1, b2, b3, t1, t2, t3, t4, last)
    return result


def solution(mesh):
    placed = (
        P("rows", None),
        P(("rows", "rep"), None, None),
        P(("rows", "rep"), None),
        P(("rows", "rep"), None),
        P(),
        P(),
        P(),
        P(None, "rep"),
        P(None, "rep"),
        P(None, "rep"),
        P(None, "rep"),
        P(),
    )
    return jax.shard_map(
        body, mesh=mesh, in_specs=placed, out_specs=P(("rows", "rep")), check_vma=False
    )
```

time: 64.6 us -> 24.9 us (0.39)
  Pallas kernels: 0 us -> 23.5 us
  blocking collectives: 15 us -> 0 us
  matrix products: 14.3 us -> 0 us
  between operations: 13.5 us -> 0.01 us
  starting transfers between devices: 13.4 us -> 0 us
  waiting for transfers between devices: 2.91 us -> 0 us
  local copies, waits for them, and re-layouts: 3.4 us -> 1.19 us
  other arithmetic: 1.49 us -> 0 us
    pallas_call x0 -> x1, Pallas kernels: none -> 23.5 us  [body(): pl.pallas_call(functools.partial(kernel, D, R), out_shape=jax.ShapeDtypeS...]
    all_gather x2 -> x0, blocking collectives: 15 us -> none  [the longest x1 7.79 us: body(): lax.all_gather(top_fourth, 'rep', axis=1, tiled=True)]
    dot_general x10 -> x0, matrix products: 14.3 us -> none  [the longest x4 7.73 us: add_block(): jnp.dot(counts.astype(jnp.bfloat16), block_table, preferred_element_type=...]
    all_to_all x2 -> x0, starting transfers between devices: 13.3 us -> none  [the longest x1 7.31 us: body(): lax.all_to_all(outgoing, 'rows', split_axis=0, concat_axis=0, tiled=True)]
    all_gather x2 -> x0, waiting for transfers between devices: 1.5 us -> none  [the longest x1 1.5 us: body(): lax.all_gather(top_third, 'rep', axis=1, tiled=True)]
    unnamed x2 -> x0, waiting for transfers between devices: 1.41 us -> none
    gather x2 -> x0, local copies, waits for them, and re-layouts: 1.13 us -> none  [interact(): pair_dots = gram_matrix[:, left_ids, right_ids]]
    unnamed x2 -> x0, other arithmetic: 0.77 us -> none
  transfers between devices with their start and end apart: 4 -> 0, of which waited for: 1 -> 0; matrix products, arithmetic and copies ran while one was open for 27% -> 0% of each run, Pallas kernels for 0% -> 0%
where the time goes in v1:
time: 24.9 us; the launch traced here: 24.7 us
  Pallas kernels  23.5 us (94%)
  local copies, waits for them, and re-layouts  1.19 us (5%)
    pallas_call x1, Pallas kernels, body(): pl.pallas_call(functools.partial(kernel, D, R), out_shape=jax.ShapeDtypeS...  23.5 us
    unnamed x1, local copies, waits for them, and re-layouts  1.19 us

profile of v1, /device:TPU:0, one launch (start us, length us, event | category | flops | bytes accessed | tf_op | source)
XLA Modules:
  0.0 24.7 jit_solution(14066319667897168285)
XLA Ops:
  0.0 23.5 %shard_map.118 = f32[16]{0:T(128)} custom-call(bf16[2048,128]{1,0:T(8,128)(2,1)} %tables.1, s32[8,8,16]{2,1,0:T(8,128)} %bitcast.4, s32[8,16]{1,0:T(8,128)} %bitcast.5, bf16[16,13]{1,0:T(8,128)(2,1)} %dense_h.1, bf16[13,512]{1,0:T(8,128)(2,1)} %bottom_first_h.1, bf16[512,256]{1,0:T(8,128)(2,1)} %bottom_second_h.1, bf16[256,128]{1,0:T(8,128)(2,1)} %bottom_third_h.1, ...), custom_call_target="tpu_custom_call" | custom-call | tf_op jit(solution)/shard_map/pallas_call | solution.py:316
  23.5 1.2 %copy.14 = f32[16]{0:T(128)} copy(f32[16]{0:T(128)} %shard_map.118) | data formatting | bytes 128

commit v2 on v1

--- a/solution.py
+++ b/solution.py
@@ -9,6 +9,7 @@
 
 TAB = 8
 HOT = 8
+LANES = 128
 MESH = pl.DeviceIdType.MESH
 BF16 = jnp.bfloat16
 F32 = jnp.float32
@@ -29,6 +30,13 @@
 
 def dot_t(a, b):
     return lax.dot_general(a, b, (((1,), (1,)), ((), ())), preferred_element_type=F32)
+
+
+def run_half(lookup, base, count):
+    if count == 4:
+        lookup(base)
+    else:
+        pl.loop(0, count // 4)(lambda g: lookup(base + 4 * g))
 
 
 def relu_round(x):
@@ -141,17 +149,11 @@
         sends.append(copy)
         return copy
 
-    first = []
-    for d in range(1, D):
-        peer = lax.rem(me + d, D)
-        first.append(
-            send(
-                out_idx.at[peer // per_table],
-                recv_idx.at[me],
-                e1_send.at[d],
-                e1_recv.at[d],
-                (peer, k),
-            )
+    first = {}
+    for d in reversed(range(1, D)):
+        peer = flip(me, d)
+        first[d] = send(
+            out_idx.at[peer // per_table], recv_idx.at[me], e1_send.at[d], e1_recv.at[d], (peer, k)
         )
     recv_idx[me] = out_idx[me // per_table]
 
@@ -207,38 +209,54 @@
     bottom_out = jnp.maximum(dot(middle, bottom_third[...]), 0.0)
 
     local[0].wait()
-    for copy in first:
-        copy.wait_recv()
 
     offset = (me % per_table) * rows
-    cells = lax.broadcasted_iota(jnp.int32, (8, rows), 1)
-
-    def group(g):
-        wanted = recv_idx[pl.ds(g * 8, 8)].reshape(8, B * HOT) - offset
-        for pair in range(B // 2):
-            halves = []
-            for b in (2 * pair, 2 * pair + 1):
-                total = jnp.zeros((8, rows), F32)
-                for s in range(HOT):
-                    j = B * s + b
-                    total = total + jnp.where(wanted[:, j : j + 1] == cells, 1.0, 0.0)
-                halves.append(total)
-            counts[16 * pair : 16 * pair + 16, :] = jnp.concatenate(halves, axis=0).astype(BF16)
+    lanes = lax.broadcasted_iota(jnp.int32, (16, LANES), 1).astype(F32).astype(BF16)
+    one, zero = jnp.ones((16, LANES), BF16), jnp.zeros((16, LANES), BF16)
+    half = B // 2
+
+    def lookup(base):
+        rows4 = recv_idx[pl.ds(base, 4)].reshape(4, B * HOT) - offset
+        wanted = jnp.concatenate([rows4, pltpu.roll(rows4, B * HOT - half, 1)], axis=0)
+        blocks = rows // LANES
+        for pair in range(half // 2):
+            totals = [jnp.zeros((16, LANES), BF16)] * blocks
+            for s in range(HOT):
+                j = B * s + 2 * pair
+                entry = jnp.concatenate([wanted[:, j : j + 1], wanted[:, j + 1 : j + 2]], axis=0)
+                entry = jnp.broadcast_to(entry, (16, LANES))
+                high_part = (entry >> 7).astype(F32).astype(BF16)
+                low_part = (entry & (LANES - 1)).astype(F32).astype(BF16)
+                hit = jnp.where(low_part == lanes, one, zero)
+                for n in range(blocks):
+                    here = jnp.where(high_part == jnp.asarray(n, BF16), hit, zero)
+                    totals[n] = totals[n] + here
+            for n in range(blocks):
+                counts[16 * pair : 16 * pair + 16, n * LANES : (n + 1) * LANES] = totals[n]
         partial = dot(counts[...], table_v[...])
-        for b in range(B):
-            part[pl.ds(g * 8, 8), b, :] = partial[8 * b : 8 * b + 8, :]
-
-    if D == 8:
-        group(0)
-    else:
-        pl.loop(0, D // 8)(group)
+        for b in range(half):
+            part[pl.ds(base, 4), b, :] = partial[8 * b : 8 * b + 4, :]
+            part[pl.ds(base, 4), b + half, :] = partial[8 * b + 4 : 8 * b + 8, :]
 
     second = []
-    for d in range(1, D):
-        peer = lax.rem(me + d, D)
+
+    def second_send(d):
+        peer = flip(me, d)
         second.append(
             send(part.at[peer], recv_pool.at[me], e2_send.at[d], e2_recv.at[d], (peer, k))
         )
+
+    low, high = D // 2, D
+    for d in range(1, low):
+        first[d].wait_recv()
+    run_half(lookup, me // low * low, low)
+    for d in range(1, low):
+        second_send(d)
+    for d in range(low, high):
+        first[d].wait_recv()
+    run_half(lookup, (1 - me // low) * low, low)
+    for d in range(low, high):
+        second_send(d)
     recv_pool[me] = part[me]
     weight_forward(0)
     for copy in second:
@@ -333,7 +351,7 @@
             pltpu.VMEM((R,) + t4.shape, BF16),
             pltpu.VMEM((TAB, 1, B * HOT), jnp.int32),
             pltpu.VMEM((D, 1, B * HOT), jnp.int32),
-            pltpu.VMEM((8 * B, tables.shape[0]), BF16),
+            pltpu.VMEM((4 * B, tables.shape[0]), BF16),
             pltpu.VMEM((D, B, E), F32),
             pltpu.VMEM((D, B, E), F32),
             pltpu.VMEM((R, B, 2 * E), BF16),

time: 24.9 us -> 24.1 us (0.968)
  Pallas kernels: 23.5 us -> 22.7 us
    pallas_call x1, Pallas kernels: 23.5 us -> 22.7 us  [body(): pl.pallas_call(functools.partial(kernel, D, R), out_shape=jax.ShapeDtypeS...]
where the time goes in v2:
time: 24.1 us; the launch traced here: 23.9 us
  Pallas kernels  22.7 us (94%)
  local copies, waits for them, and re-layouts  1.19 us (5%)
    pallas_call x1, Pallas kernels, body(): pl.pallas_call(functools.partial(kernel, D, R), out_shape=jax.ShapeDtypeS...  22.7 us
    unnamed x1, local copies, waits for them, and re-layouts  1.19 us

profile of v2, /device:TPU:0, one launch (start us, length us, event | category | flops | bytes accessed | tf_op | source)
XLA Modules:
  0.0 23.9 jit_solution(6477466835330951116)
XLA Ops:
  0.0 22.7 %shard_map.118 = f32[16]{0:T(128)} custom-call(bf16[2048,128]{1,0:T(8,128)(2,1)} %tables.1, s32[8,8,16]{2,1,0:T(8,128)} %bitcast.4, s32[8,16]{1,0:T(8,128)} %bitcast.5, bf16[16,13]{1,0:T(8,128)(2,1)} %dense_h.1, bf16[13,512]{1,0:T(8,128)(2,1)} %bottom_first_h.1, bf16[512,256]{1,0:T(8,128)(2,1)} %bottom_second_h.1, bf16[256,128]{1,0:T(8,128)(2,1)} %bottom_third_h.1, ...), custom_call_target="tpu_custom_call" | custom-call | tf_op jit(solution)/shard_map/pallas_call | solution.py:334
  22.7 1.2 %copy.14 = f32[16]{0:T(128)} copy(f32[16]{0:T(128)} %shard_map.118) | data formatting | bytes 128
